TPU v7x, 32 devices: a whole 2x2x4 slice. The times are simulated.
32 devices in a mesh: dp: 4 (over z), bal: 4 (over x, core), tensor: 2 (over y).
Axes of the slice: x: 2, y: 2, z: 4, core: 2. Of those that a mesh axis runs over, the one named last changes fastest.
Arguments:
- tiles: bfloat16 [4, 4, 16, 1280, 128], P('dp', 'bal', None, 'tensor'), may hold values from -6 to 6
- tile_counts: int32 [4, 4], P('dp'), may hold values from 1 to 16, 32 in all within a row
- doc_order: int32 [4, 4], P('dp'), may hold values from 0 to 3, each once within a row
- qkv_weight: bfloat16 [3, 1280, 1280], P(None, 'dp', 'tensor'), may hold values from -6 to 6
- out_weight: bfloat16 [1280, 1280], P('dp', 'tensor'), may hold values from -0.625 to 0.625
Outputs:
- encoded: bfloat16 [4, 32, 1280, 128], P('dp', 'bal', 'tensor')
Inputs may be any that keep to these rules, and one draw needn't show every extreme that they name: `tile_counts`: each row sums to 32, and in every row some document has exactly 16 tiles. `doc_order`: each row names every document once.
All inputs are finite; a program needn't handle non-finite values.
Results may differ from a plain program's by a relative error of at most 0.012.
Values may be sent and summed in bfloat16 or wider, within the bound.
A program may use at most 64 MiB of HBM per device.

v0:
```python
import jax
import jax.numpy as jnp
from jax import lax
from jax.sharding import PartitionSpec as P

HDIM = 80
CAP = 8


EPSILON = 1e-06


def layout(counts, ordering):
    doc_ids = jnp.arange(counts.shape[0], dtype=jnp.int32)
    position = jnp.sum(
        jnp.where(ordering[None, :] == doc_ids[:, None], doc_ids[None, :], 0), axis=1
    )
    starts = jnp.sum(jnp.where(position[None, :] < position[:, None], counts[None, :], 0), axis=1)
    return (doc_ids, starts)


def normalize(tile_rows):
    values = tile_rows.astype(jnp.float32)
    center = values - jnp.mean(values, axis=1, keepdims=True)
    spread = jnp.mean(center * center, axis=1, keepdims=True)
    return (center * lax.rsqrt(spread + EPSILON)).astype(jnp.bfloat16)


def local(tiles, tile_counts, doc_order, qkv_weight, out_weight):
    bal_size = lax.axis_size("bal")
    owner_idx = lax.axis_index("bal")
    counts = tile_counts[0]
    doc_ids, starts = layout(counts, doc_order[0])
    own_tiles = tiles[0, 0]
    slot_count, slices, patches = own_tiles.shape
    pair_count = slot_count // bal_size
    own_start = jnp.sum(jnp.where(doc_ids == owner_idx, starts, 0))
    own_count = jnp.sum(jnp.where(doc_ids == owner_idx, counts, 0))
    target_dev = jnp.arange(bal_size, dtype=jnp.int32)[:, None]
    pair_rank = jnp.arange(pair_count, dtype=jnp.int32)[None, :]
    tile_pick = (pair_rank * bal_size + (target_dev - own_start) % bal_size).reshape(-1)
    is_live = (tile_pick < own_count).astype(jnp.bfloat16)
    outbound = jnp.take(own_tiles, tile_pick, axis=0) * is_live[:, None, None]
    outbound = outbound.reshape(bal_size, pair_count, slices * patches)
    arrived = lax.all_to_all(outbound, "bal", split_axis=0, concat_axis=0, tiled=True)
    arrived = arrived.reshape(bal_size * pair_count, slices, patches)
    packed = jnp.arange(CAP, dtype=jnp.int32) * bal_size + owner_idx
    inside = (starts[None, :] <= packed[:, None]) & (packed[:, None] < (starts + counts)[None, :])
    source = jnp.sum(jnp.where(inside, doc_ids[None, :], 0), axis=1)
    offset = packed - jnp.sum(jnp.where(inside, starts[None, :], 0), axis=1)
    chosen = jnp.take(arrived, source * pair_count + offset // bal_size, axis=0)
    gathered = lax.all_gather(chosen, "tensor", axis=1, tiled=True)
    normed = normalize(gathered)
    full_qkv, full_out = (
        lax.all_gather(qkv_weight, "dp", axis=1, tiled=True),
        lax.all_gather(out_weight, "dp", axis=0, tiled=True),
    )
    projected = jnp.einsum("cdp,kdf->kcfp", normed, full_qkv, preferred_element_type=jnp.float32)
    head_count = slices // HDIM
    projected = projected.astype(jnp.bfloat16).reshape(3, CAP, head_count, HDIM, patches)
    scores = jnp.einsum(
        "rhet,rhes->rhts", projected[0], projected[1], preferred_element_type=jnp.float32
    ) * HDIM ** (-0.5)
    probs = jax.nn.softmax(scores, axis=-1).astype(jnp.bfloat16)
    context = jnp.einsum("rhts,rhes->rhet", probs, projected[2], preferred_element_type=jnp.float32)
    context = context.astype(jnp.bfloat16).reshape(CAP, slices, patches)
    partial_value = jnp.einsum("cep,fe->cfp", context, full_out, preferred_element_type=jnp.float32)
    summed = lax.psum_scatter(
        partial_value.astype(jnp.bfloat16), "tensor", scatter_dimension=1, tiled=True
    ).astype(jnp.float32)
    encoded = (chosen.astype(jnp.float32) + summed).astype(jnp.bfloat16)
    encoded = encoded.reshape(CAP, slices * patches)
    pair_back = max(1, CAP // bal_size)
    back_rank = jnp.arange(pair_back, dtype=jnp.int32)[None, :]
    residue = (owner_idx - target_dev * CAP) % bal_size
    within = back_rank * bal_size + residue
    is_valid = within < CAP
    enc_slot = jnp.where(is_valid, (target_dev * CAP + within - owner_idx) // bal_size, 0).reshape(
        -1
    )
    outgoing = (
        jnp.take(encoded, enc_slot, axis=0) * is_valid.reshape(-1).astype(jnp.bfloat16)[:, None]
    )
    outgoing = outgoing.reshape(bal_size, pair_back, slices * patches)
    returned = lax.all_to_all(outgoing, "bal", split_axis=0, concat_axis=0, tiled=True)
    returned = returned.reshape(bal_size * pair_back, slices * patches)
    final_slot = jnp.arange(CAP, dtype=jnp.int32)
    final_pos = owner_idx * CAP + final_slot
    gather_idx = final_pos % bal_size * pair_back + final_slot // bal_size
    result = jnp.take(returned, gather_idx, axis=0).reshape(1, CAP, slices, patches)
    return result


def solution(mesh):
    placed = (
        P("dp", "bal", None, "tensor", None),
        P("dp", None),
        P("dp", None),
        P(None, "dp", "tensor"),
        P("dp", "tensor"),
    )
    return jax.shard_map(
        local, mesh=mesh, in_specs=placed, out_specs=P("dp", "bal", "tensor", None), check_vma=False
    )
```

profile of v0, /device:TPU:0, one launch (start us, length us, event | category | flops | bytes accessed | tf_op | source)
XLA Modules:
  0.0 325.9 jit_solution(6447347052396666798)
XLA Ops:
  8.3 1.4 fusion.28
  11.3 2.4 gather_fusion
  13.7 3.0 gather.14
  16.6 2.8 select_multiply_fusion
  19.4 4.4 %all-to-all-start = ((bf16[4,4,81920]{2,1,0:T(4,128)(2,1)}), bf16[4,4,81920]{2,1,0:T(4,128)(2,1)S(1)}, u32[]{:S(2)}, u32[]{:S(2)}) async-start(bf16[4,4,81920]{2,1,0:T(4,128)(2,1)} %select_multiply_fusion), calls=%async_computation | async-start | bytes 5242880 | tf_op jit(solution)/shard_map/all_to_all | solution.py:45
  24.0 31.2 %all-to-all-done = bf16[4,4,81920]{2,1,0:T(4,128)(2,1)S(1)} async-done(((bf16[4,4,81920]{2,1,0:T(4,128)(2,1)}), bf16[4,4,81920]{2,1,0:T(4,128)(2,1)S(1)}, u32[]{:S(2)}, u32[]{:S(2)}) %all-to-all-start) | async-done | bytes 2621472 | tf_op jit(solution)/shard_map/all_to_all | solution.py:45
  55.1 3.7 %reshape.273 = bf16[16,640,128]{2,1,0:T(8,128)(2,1)} reshape(bf16[4,4,81920]{2,1,0:T(4,128)(2,1)S(1)} %all-to-all-done) | data formatting | bytes 5242880 | tf_op jit(solution)/shard_map/reshape | solution.py:46
  58.8 2.5 gather_fusion.1
  61.4 1.2 broadcast_select_fusion
  64.4 38.6 %all-gather.4.cloned.1.call-done = bf16[8,1280,128]{2,1,0:T(8,128)(2,1)} async-done(((bf16[8,640,128]{2,1,0:T(8,128)(2,1)}), bf16[8,1280,128]{2,1,0:T(8,128)(2,1)}) %all-gather.4.cloned.1.call-update) | async-done | bytes 2621456 | tf_op jit(solution)/shard_map/all_gather | solution.py:52
  102.9 2.2 convert_reduce_fusion
  106.2 91.0 %all-gather.6.cloned.1.call-done = bf16[3,1280,640]{2,1,0:T(8,128)(2,1)} async-done(((bf16[3,320,640]{2,1,0:T(8,128)(2,1)}), bf16[3,1280,640]{2,1,0:T(8,128)(2,1)}) %all-gather.6.cloned.1.call-update) | async-done | bytes 4915216 | tf_op jit(solution)/shard_map/all_gather | solution.py:55
  197.2 8.7 %convert_bitcast_fusion = bf16[3,8,640,128]{2,3,0,1:T(8,128)(2,1)S(1)} fusion(bf16[3,1280,640]{2,1,0:T(8,128)(2,1)} %all-gather.6.cloned.1.call-done, bf16[8,1280,128]{2,1,0:T(8,128)(2,1)} %all-gather.4.cloned.1.call-done, f32[8,128]{1,0:T(8,128)S(1)} %add_rsqrt_fusion, f32[8,128]{1,0:T(8,128)S(1)} %broadcast_multiply_fusion), kind=kOutput, calls=%fused_computation.15 | convolution fusion | flops 5040373760 | bytes 11476992 | tf_op jit(solution)/shard_map/cdp,kdf->kcfp/dot_general | solution.py:58
  205.9 2.1 fusion.38
  208.0 2.4 copy.30
  210.4 2.4 copy.31
  212.8 1.5 copy.29
  214.3 5.4 %fusion.39 = (f32[8,8,128]{2,1,0:T(8,128)S(1)}, f32[8,8,128,128]{2,3,1,0:T(8,128)}) fusion(bf16[8,8,80,128]{3,2,1,0:T(8,128)(2,1)} %bitcast.74, bf16[8,8,80,128]{3,2,1,0:T(8,128)(2,1)} %bitcast.75), kind=kOutput, calls=%fused_computation.109 | convolution fusion | flops 170918016 | bytes 6848512 | tf_op jit(solution)/shard_map/sub | solution.py:64
  219.7 4.1 %fusion.22 = bf16[8,8,80,128]{3,2,1,0:T(8,128)(2,1)} fusion(bf16[8,8,80,128]{3,2,1,0:T(8,128)(2,1)S(1)} %bitcast.76, f32[8,8,128,128]{2,3,1,0:T(8,128)} %get-tuple-element.17, f32[8,8,128]{2,1,0:T(8,128)S(1)} %get-tuple-element.16), kind=kOutput, calls=%fused_computation.29 | convolution fusion | flops 170524672 | bytes 6848512 | tf_op jit(solution)/shard_map/rhts,rhes->rhet/dot_general | solution.py:65
  223.8 11.5 %all-gather.8.cloned.1.call-done = bf16[1280,640]{1,0:T(8,128)(2,1)} async-done(((bf16[320,640]{1,0:T(8,128)(2,1)}), bf16[1280,640]{1,0:T(8,128)(2,1)}) %all-gather.8.cloned.1.call-update) | async-done | bytes 1638416 | tf_op jit(solution)/shard_map/all_gather | solution.py:56
  235.3 5.6 %fusion.8 = bf16[8,1280,128]{1,2,0:T(8,128)(2,1)} fusion(bf16[8,640,128]{2,1,0:T(8,128)(2,1)} %bitcast.79, bf16[1280,640]{1,0:T(8,128)(2,1)} %all-gather.8.cloned.1.call-done), kind=kOutput, calls=%fused_computation.19 | convolution fusion | flops 1679032320 | bytes 5570560 | tf_op jit(solution)/shard_map/cep,fe->cfp/dot_general | solution.py:67
  240.8 4.8 %copy.41 = bf16[8,1280,128]{2,0,1:T(8,128)(2,1)} copy(bf16[8,1280,128]{1,2,0:T(8,128)(2,1)} %fusion.8) | data formatting | bytes 5242880
  245.6 3.9 %copy.50 = bf16[160,8,8,128]{3,1,2,0:T(8,128)(2,1)} copy(bf16[160,8,8,128]{3,2,1,0:T(8,128)(2,1)} %bitcast.71) | data formatting | bytes 5242880
  250.0 36.3 %reduce-scatter.4.cloned.1.call-done = bf16[640,1024]{1,0:T(8,128)(2,1)} async-done(((bf16[1280,1024]{1,0:T(8,128)(2,1)}), bf16[640,1024]{1,0:T(8,128)(2,1)}) %reduce-scatter.4.cloned.1.call-update) | async-done | bytes 1310736
  286.2 1.7 copy.45
  289.2 1.4 gather_fusion.2
  290.8 1.9 reshape.276
  292.7 3.5 %all-to-all-start.1 = ((bf16[4,2,81920]{2,1,0:T(2,128)(2,1)}), bf16[4,2,81920]{2,1,0:T(2,128)(2,1)S(1)}, u32[]{:S(2)}, u32[]{:S(2)}) async-start(bf16[4,2,81920]{2,1,0:T(2,128)(2,1)} %reshape.276), calls=%async_computation.1 | async-start | bytes 2621440 | tf_op jit(solution)/shard_map/all_to_all | solution.py:85
  296.3 17.2 %all-to-all-done.1 = bf16[4,2,81920]{2,1,0:T(2,128)(2,1)S(1)} async-done(((bf16[4,2,81920]{2,1,0:T(2,128)(2,1)}), bf16[4,2,81920]{2,1,0:T(2,128)(2,1)S(1)}, u32[]{:S(2)}, u32[]{:S(2)}) %all-to-all-start.1) | async-done | bytes 1310752 | tf_op jit(solution)/shard_map/all_to_all | solution.py:85
  314.0 2.5 gather_fusion.3
  316.4 1.6 select_bitcast_fusion
  318.1 1.3 copy.35
  (52 shorter events, 8.6 us)
Async XLA Ops:
  6.5 4.7 %copy-start = (bf16[1,1,16,640,128]{4,3,2,1,0:T(8,128)(2,1)S(1)}, bf16[1,1,16,640,128]{4,3,2,1,0:T(8,128)(2,1)}, u32[]{:S(2)}) copy-start(bf16[1,1,16,640,128]{4,3,2,1,0:T(8,128)(2,1)} %param.7) | copy-start | bytes 7864324
  19.4 4.4 %copy-start.4 = (s32[1,4]{1,0:T(1,128)S(1)}, s32[1,4]{1,0:T(1,128)}, u32[]{:S(2)}) copy-start(s32[1,4]{1,0:T(1,128)} %param.8) | copy-start | bytes 52
  19.4 35.7 %all-to-all-start = ((bf16[4,4,81920]{2,1,0:T(4,128)(2,1)}), bf16[4,4,81920]{2,1,0:T(4,128)(2,1)S(1)}, u32[]{:S(2)}, u32[]{:S(2)}) async-start(bf16[4,4,81920]{2,1,0:T(4,128)(2,1)} %select_multiply_fusion), calls=%async_computation | async-start | bytes 5242880 | tf_op jit(solution)/shard_map/all_to_all | solution.py:45
  23.8 79.1 %all-gather.4.cloned.1.call-start = ((), (), s32[]{:S(2)}) async-start(), calls=%async_computation.3 | async-start | bytes 3932160 | tf_op jit(solution)/shard_map/all_gather | solution.py:52
  62.7 134.5 %all-gather.6.cloned.1.call-start = ((), (), s32[]{:S(2)}) async-start(), calls=%async_computation.4 | async-start | bytes 6144000 | tf_op jit(solution)/shard_map/all_gather | solution.py:55
  63.4 171.9 %all-gather.8.cloned.1.call-start = ((), (), s32[]{:S(2)}) async-start(), calls=%async_computation.5 | async-start | bytes 2048000 | tf_op jit(solution)/shard_map/all_gather | solution.py:56
  64.1 222.1 %reduce-scatter.4.cloned.1.call-start = ((), (), s32[]{:S(2)}) async-start(), calls=%async_computation.6 | async-start | bytes 3932160
  102.9 2.5 copy-start.2
  214.3 5.4 %copy-start.3 = (bf16[1,8,640,128]{3,2,1,0:T(8,128)(2,1)S(1)}, bf16[1,8,640,128]{3,2,1,0:T(8,128)(2,1)}, u32[]{:S(2)}) copy-start(bf16[1,8,640,128]{3,2,1,0:T(8,128)(2,1)} %copy.29) | copy-start | bytes 3932164
  292.7 20.8 %all-to-all-start.1 = ((bf16[4,2,81920]{2,1,0:T(2,128)(2,1)}), bf16[4,2,81920]{2,1,0:T(2,128)(2,1)S(1)}, u32[]{:S(2)}, u32[]{:S(2)}) async-start(bf16[4,2,81920]{2,1,0:T(2,128)(2,1)} %reshape.276), calls=%async_computation.1 | async-start | bytes 2621440 | tf_op jit(solution)/shard_map/all_to_all | solution.py:85
  316.4 2.9 copy-start.1
Sparse Core Ops, SparseCore 0:
  62.8 40.1 all-gather.3
  104.5 92.6 all-gather.5
  198.7 36.4 all-gather.7
  249.7 36.5 reduce-scatter.3
where the time goes:
time: 327 us; the launch traced here: 326 us
  waiting for transfers between devices  227 us (69%)
  local copies, waits for them, and re-layouts  39.3 us (12%)
  matrix products  23.8 us (7%)
  other arithmetic  14.2 us (4%)
  between operations  13.3 us (4%)
  starting transfers between devices  8.21 us (3%)
    all_gather x1, waiting for transfers between devices, local(): lax.all_gather(qkv_weight, 'dp', axis=1, tiled=True)  91 us
    all_gather x1, waiting for transfers between devices, local(): gathered = lax.all_gather(chosen, 'tensor', axis=1, tiled=True)  38.6 us
    unnamed x5, waiting for transfers between devices  37.7 us
    all_to_all x1, waiting for transfers between devices, local(): lax.all_to_all(outbound, 'bal', split_axis=0, concat_axis=0, tiled=True)  31.2 us
    all_to_all x1, waiting for transfers between devices, local(): lax.all_to_all(outgoing, 'bal', split_axis=0, concat_axis=0, tiled=True)  17.2 us
    unnamed x14, local copies, waits for them, and re-layouts  11.5 us
    all_gather x1, waiting for transfers between devices, local(): lax.all_gather(out_weight, 'dp', axis=0, tiled=True)  11.5 us
    dot_general x1, matrix products, local(): jnp.einsum('cdp,kdf->kcfp', normed, full_qkv, preferred_element_type=jnp....  8.69 us
  transfers between devices with their start and end apart: 6, of which 6 were waited for; matrix products, arithmetic and copies ran while one was open for 9% of the time, Pallas kernels for 0%

commit v1 on v0

v1 whole, which is shorter than its diff:
```python
import functools

import jax
import jax.numpy as jnp
from jax import lax
from jax.experimental import pallas as pl
from jax.experimental.pallas import tpu as pltpu
from jax.sharding import PartitionSpec as P

HDIM = 80
CAP = 8
CHUNK = 2
EPSILON = 1e-06
MESH = pl.DeviceIdType.MESH


def flip(index, bit):
    return index + bit - 2 * bit * ((index // bit) % 2)


def bits_of(size):
    bits = []
    while 1 << len(bits) < size:
        bits.append(1 << len(bits))
    return bits


def remote(src, dst, send, recv, **device):
    return pltpu.make_async_remote_copy(
        src_ref=src, dst_ref=dst, send_sem=send, recv_sem=recv, device_id=device, device_id_type=MESH
    )


def gather_kernel(sizes, *refs):
    nd, nb, nt = sizes
    bits = bits_of(nb)
    ns = len(bits)
    tab, tiles, wq_in, wo_in, gath, wq, wo = refs[:7]
    sends, recvs = refs[7 : 7 + ns], refs[7 + ns : 7 + 2 * ns]
    t_send, t_recv, y_send, y_recv, w_send, w_recv, d_send, d_recv = refs[7 + 2 * ns :]
    z, b, t = lax.axis_index("dp"), lax.axis_index("bal"), lax.axis_index("tensor")
    slices = tiles.shape[1]
    chunks = CAP // CHUNK

    barrier = pltpu.get_barrier_semaphore()
    for m in bits:
        pl.semaphore_signal(barrier, inc=1, device_id={"bal": flip(b, m)}, device_id_type=MESH)
    for j in range(1, nt):
        pl.semaphore_signal(barrier, inc=1, device_id={"tensor": (t + j) % nt}, device_id_type=MESH)

    def greet(j, carry):
        pl.semaphore_signal(barrier, inc=1, device_id={"dp": (z + j) % nd}, device_id_type=MESH)
        return carry

    lax.fori_loop(1, nd, greet, 0)
    pl.semaphore_wait(barrier, ns + nt - 1 + nd - 1)

    pairs = ((wq_in, wq), (wo_in, wo))

    def spread(j, a):
        src, dst = pairs[a]
        return remote(
            src.at[b], dst.at[z, b], w_send.at[a, j], w_recv.at[a, j], dp=(z + j) % nd
        )

    for a in range(2):

        def start_spread(j, carry, a=a):
            spread(j, a).start()
            return carry

        lax.fori_loop(1, nd, start_spread, 0)

    def tile_copy(s, slot, c):
        part = pl.ds(c * CHUNK, CHUNK)
        return remote(
            sends[s].at[slot, part],
            recvs[s].at[slot, part],
            t_send.at[s, slot, c],
            t_recv.at[s, slot, c],
            bal=flip(b, bits[s]),
        )

    def slot_of(s, r):
        return r >> (s + 1)

    def wait_for(s, r, c):
        for q in range(s):
            tile_copy(q, slot_of(q, r), c).wait_recv()

    def current(s, r, i):
        value = tiles[tab[0, r * CAP + i]]
        for q in range(s):
            value = lax.select(
                tab[1 + q, r * CAP + i] != 0, recvs[q][slot_of(q, r), i], value
            )
        return value

    for s, m in enumerate(bits):
        wanted = [r for r in range(nb) if r & (m - 1) == 0 and r & m]
        for r in reversed(wanted):
            slot = slot_of(s, r - m)
            for c in range(chunks):
                wait_for(s, r, c)

                def fill(i, carry, s=s, r=r, slot=slot):
                    sends[s][slot, i] = current(s, r, i)
                    return carry

                lax.fori_loop(c * CHUNK, (c + 1) * CHUNK, fill, 0)
                tile_copy(s, slot, c).start()

    mine = pl.ds(pl.multiple_of(t * slices, 16), slices)

    def y_copy(c, j):
        part = gath.at[pl.ds(c * CHUNK, CHUNK), mine, :]
        return remote(part, part, y_send.at[c, j], y_recv.at[c, j], tensor=(t + j) % nt)

    for c in range(chunks):
        wait_for(ns, 0, c)

        def settle(i, carry):
            gath[i, mine, :] = current(ns, 0, i)
            return carry

        lax.fori_loop(c * CHUNK, (c + 1) * CHUNK, settle, 0)
        for j in range(1, nt):
            y_copy(c, j).start()

    for a in range(2):
        src, dst = pairs[a]
        dst[z] = src[...]

    def doubled(j, a, s, e):
        src = (z + nd - j) % nd
        held = b
        for q in range(s):
            if (e >> q) & 1:
                held = flip(held, bits[ns - 1 - q])
        dst = pairs[a][1].at[src, held]
        at = (1 << s) - 1 + e
        return remote(
            dst, dst, d_send.at[a, j, at], d_recv.at[a, j, at], bal=flip(b, bits[ns - 1 - s])
        )

    for a in range(2):

        def first(j, carry, a=a):
            spread(j, a).wait_recv()
            doubled(j, a, 0, 0).start()
            return carry

        lax.fori_loop(1, nd, first, 0)
    for s in range(1, ns + 1):
        for a in range(2):

            def further(j, carry, a=a, s=s):
                for e in range(1 << (s - 1)):
                    doubled(j, a, s - 1, e).wait_recv()
                if s < ns:
                    for e in range(1 << s):
                        doubled(j, a, s, e).start()
                return carry

            lax.fori_loop(1, nd, further, 0)

    for c in range(chunks):
        for j in range(1, nt):
            y_copy(c, j).wait_recv()
            y_copy(c, j).wait_send()
    for s, m in enumerate(bits):
        for slot in range(nb >> (s + 1)):
            for c in range(chunks):
                tile_copy(s, slot, c).wait_send()
    for a in range(2):

        def drain(j, carry, a=a):
            spread(j, a).wait_send()
            for s in range(ns):
                for e in range(1 << s):
                    doubled(j, a, s, e).wait_send()
            return carry

        lax.fori_loop(1, nd, drain, 0)


def gather_all(table, tiles, qkv_weight, out_weight):
    nd, nb, nt = (lax.axis_size(name) for name in ("dp", "bal", "tensor"))
    ns = len(bits_of(nb))
    slots, slices, patches = tiles.shape
    columns = qkv_weight.shape[-1]
    wq = qkv_weight.reshape(nb, -1, columns)
    wo = out_weight.reshape(nb, -1, columns)
    chunks = CAP // CHUNK
    dtype = tiles.dtype
    vmem = pl.BlockSpec(memory_space=pltpu.VMEM)
    dma = pltpu.SemaphoreType.DMA
    buffers = [pltpu.VMEM((nb >> (s + 1), CAP, slices, patches), dtype) for s in range(ns)]
    gathered, full_qkv, full_out = pl.pallas_call(
        functools.partial(gather_kernel, (nd, nb, nt)),
        out_shape=(
            jax.ShapeDtypeStruct((CAP, nt * slices, patches), dtype),
            jax.ShapeDtypeStruct((nd,) + wq.shape, dtype),
            jax.ShapeDtypeStruct((nd,) + wo.shape, dtype),
        ),
        in_specs=[pl.BlockSpec(memory_space=pltpu.SMEM), vmem, vmem, vmem],
        out_specs=(vmem, vmem, vmem),
        scratch_shapes=buffers
        + buffers
        + [dma((ns, max(nb // 2, 1), chunks))] * 2
        + [dma((chunks, nt))] * 2
        + [dma((2, nd))] * 2
        + [dma((2, nd, nb))] * 2,
        compiler_params=pltpu.CompilerParams(
            collective_id=0, has_side_effects=True, vmem_limit_bytes=50 * 1024 * 1024
        ),
        name="gather_all",
    )(table, tiles, wq, wo)
    return (
        gathered,
        full_qkv.reshape((nd,) + qkv_weight.shape),
        full_out.reshape((-1, columns)),
    )


def route(counts, ordering, slot_count):
    nb, b = lax.axis_size("bal"), lax.axis_index("bal")
    doc_ids = jnp.arange(counts.shape[0], dtype=jnp.int32)
    position = jnp.sum(
        jnp.where(ordering[None, :] == doc_ids[:, None], doc_ids[None, :], 0), axis=1
    )
    starts = jnp.sum(jnp.where(position[None, :] < position[:, None], counts[None, :], 0), axis=1)
    own_start = jnp.sum(jnp.where(doc_ids == b, starts, 0))
    relative = jnp.arange(nb * CAP, dtype=jnp.int32)
    packed = ((relative // CAP) ^ b) * CAP + relative % CAP
    inside = (starts[:, None] <= packed[None, :]) & (packed[None, :] < (starts + counts)[:, None])
    owner = jnp.sum(jnp.where(inside, doc_ids[:, None], 0), axis=0)
    rows = [jnp.clip(packed - own_start, 0, slot_count - 1)]
    for m in bits_of(nb):
        rows.append(((owner ^ b) // m) % 2)
    return jnp.stack(rows)


def normalize(tile_rows):
    values = tile_rows.astype(jnp.float32)
    center = values - jnp.mean(values, axis=1, keepdims=True)
    spread = jnp.mean(center * center, axis=1, keepdims=True)
    return (center * lax.rsqrt(spread + EPSILON)).astype(jnp.bfloat16)


def local(tiles, tile_counts, doc_order, qkv_weight, out_weight):
    own_tiles = tiles[0, 0]
    slot_count, slices, patches = own_tiles.shape
    table = route(tile_counts[0], doc_order[0], slot_count)
    gathered, full_qkv, full_out = gather_all(table, own_tiles, qkv_weight, out_weight)
    t = lax.axis_index("tensor")
    chosen = lax.dynamic_slice_in_dim(gathered, t * slices, slices, axis=1)
    normed = normalize(gathered)
    full_qkv = full_qkv.transpose(1, 0, 2, 3).reshape(3, -1, slices)
    projected = jnp.einsum("cdp,kdf->kcfp", normed, full_qkv, preferred_element_type=jnp.float32)
    head_count = slices // HDIM
    projected = projected.astype(jnp.bfloat16).reshape(3, CAP, head_count, HDIM, patches)
    scores = jnp.einsum(
        "rhet,rhes->rhts", projected[0], projected[1], preferred_element_type=jnp.float32
    ) * HDIM ** (-0.5)
    probs = jax.nn.softmax(scores, axis=-1).astype(jnp.bfloat16)
    context = jnp.einsum("rhts,rhes->rhet", probs, projected[2], preferred_element_type=jnp.float32)
    context = context.astype(jnp.bfloat16).reshape(CAP, slices, patches)
    partial_value = jnp.einsum("cep,fe->cfp", context, full_out, preferred_element_type=jnp.float32)
    summed = lax.psum_scatter(
        partial_value.astype(jnp.bfloat16), "tensor", scatter_dimension=1, tiled=True
    ).astype(jnp.float32)
    return (chosen.astype(jnp.float32) + summed).astype(jnp.bfloat16)[None]


def solution(mesh):
    placed = (
        P("dp", "bal", None, "tensor", None),
        P("dp", None),
        P("dp", None),
        P(None, "dp", "tensor"),
        P("dp", "tensor"),
    )
    return jax.shard_map(
        local, mesh=mesh, in_specs=placed, out_specs=P("dp", "bal", "tensor", None), check_vma=False
    )
```

time: 327 us -> 155 us (0.47)
  waiting for transfers between devices: 227 us -> 36.2 us
  Pallas kernels: 0 us -> 72.1 us
  local copies, waits for them, and re-layouts: 39.3 us -> 7.23 us
  starting transfers between devices: 8.21 us -> 0.01 us
  other arithmetic: 14.2 us -> 7.42 us
  matrix products: 23.8 us -> 17.7 us
    all_gather x3 -> x0, waiting for transfers between devices: 141 us -> none  [the longest x1 91 us: local(): lax.all_gather(qkv_weight, 'dp', axis=1, tiled=True)]
    pallas_call x0 -> x1, Pallas kernels: none -> 72.1 us  [gather_all(): pl.pallas_call(functools.partial(gather_kernel, (nd, nb, nt)), out_shape=...]
    all_to_all x2 -> x0, waiting for transfers between devices: 48.3 us -> none  [the longest x1 31.2 us: local(): lax.all_to_all(outbound, 'bal', split_axis=0, concat_axis=0, tiled=True)]
    unnamed x5 -> x1, waiting for transfers between devices: 37.7 us -> 0.02 us
    reduce_scatter x0 -> x1, waiting for transfers between devices: none -> 36.2 us  [local(): lax.psum_scatter(partial_value.astype(jnp.bfloat16), 'tensor', scatter_di...]
    gather x5 -> x0, local copies, waits for them, and re-layouts: 11.8 us -> none  [the longest x2 5.35 us: local(): outbound = jnp.take(own_tiles, tile_pick, axis=0) * is_live[:, None, None]]
    unnamed x14 -> x8, local copies, waits for them, and re-layouts: 11.5 us -> 2.49 us
    all_to_all x2 -> x0, starting transfers between devices: 7.91 us -> none  [the longest x1 4.37 us: local(): lax.all_to_all(outbound, 'bal', split_axis=0, concat_axis=0, tiled=True)]
  transfers between devices with their start and end apart: 6 -> 1, of which waited for: 6 -> 1; matrix products, arithmetic and copies ran while one was open for 9% -> 0% of each run, Pallas kernels for 0% -> 0%
where the time goes in v1:
time: 155 us; the launch traced here: 154 us
  Pallas kernels  72.1 us (47%)
  waiting for transfers between devices  36.2 us (23%)
  matrix products  17.7 us (11%)
  between operations  13.5 us (9%)
  other arithmetic  7.42 us (5%)
  local copies, waits for them, and re-layouts  7.23 us (5%)
    pallas_call x1, Pallas kernels, gather_all(): pl.pallas_call(functools.partial(gather_kernel, (nd, nb, nt)), out_shape=...  72.1 us
    reduce_scatter x1, waiting for transfers between devices, local(): lax.psum_scatter(partial_value.astype(jnp.bfloat16), 'tensor', scatter_di...  36.2 us
    dot_general x1, matrix products, local(): jnp.einsum('cdp,kdf->kcfp', normed, full_qkv, preferred_element_type=jnp....  5.57 us
    sub x1, matrix products, local(): probs = jax.nn.softmax(scores, axis=-1).astype(jnp.bfloat16)  5.35 us
    dot_general x1, matrix products, local(): jnp.einsum('cep,fe->cfp', context, full_out, preferred_element_type=jnp.f...  3.72 us
  transfers between devices with their start and end apart: 1, of which 1 were waited for; matrix products, arithmetic and copies ran while one was open for 0% of the time, Pallas kernels for 0%

profile of v1, /device:TPU:0, one launch (start us, length us, event | category | flops | bytes accessed | tf_op | source)
XLA Modules:
  0.0 154.1 jit_solution(753314335191350185)
XLA Ops:
  6.5 0.0 reduce-scatter.2.cloned.1.call-start
  6.5 0.8 select_reduce_fusion.2
  7.3 0.8 select_reduce_fusion.1
  8.2 1.3 fusion.30
  9.4 0.1 select_reduce_fusion
  9.5 0.7 and_select_fusion.2
  10.2 0.0 copy-start
  10.2 1.3 copy-done
  11.5 0.0 copy-start.1
  11.5 1.0 copy-done.1
  12.5 72.1 %gather_all.1 = (bf16[8,1280,128]{2,1,0:T(8,128)(2,1)}, bf16[4,4,240,640]{3,2,1,0:T(8,128)(2,1)}, bf16[4,4,80,640]{3,2,1,0:T(8,128)(2,1)S(1)}) custom-call(s32[3,32]{1,0:T(4,128)S(1)} %pad_add_fusion.refs_0_, bf16[16,640,128]{2,1,0:T(8,128)(2,1)} %bitcast.62, bf16[4,240,640]{2,1,0:T(8,128)(2,1)S(1)} %bitcast.57, bf16[4,80,640]{2,1,0:T(8,128)(2,1)S(1)} %bitcast.58), custom_call_target="tpu_custom_call" | custom-call | tf_op jit(solution)/shard_map/gather_all/pallas_call | solution.py:199
  84.6 0.0 copy-start.2
  84.6 3.0 %copy.11 = bf16[4,3,320,640]{3,2,0,1:T(8,128)(2,1)S(1)} copy(bf16[4,3,320,640]{3,2,1,0:T(8,128)(2,1)} %bitcast.61) | data formatting | bytes 9830400 | tf_op jit(solution)/shard_map/reshape | solution.py:221
  87.6 0.2 copy-done.2
  87.9 0.3 convert_reduce_fusion
  88.2 0.7 fusion.3
  88.9 5.6 %convert_bitcast_fusion = bf16[3,8,640,128]{3,2,1,0:T(8,128)(2,1)S(1)} fusion(bf16[3,1280,640,1]{2,1,3,0:T(8,128)(2,1)S(1)} %bitcast.60, bf16[8,1280,128]{2,1,0:T(8,128)(2,1)S(1)} %copy-done.2, f32[8,128]{1,0:T(8,128)S(1)} %add_rsqrt_fusion, f32[8,128]{1,0:T(8,128)S(1)} %broadcast_multiply_fusion), kind=kOutput, calls=%fused_computation.9 | convolution fusion | flops 5040373760 | bytes 11476992 | tf_op jit(solution)/shard_map/cdp,kdf->kcfp/dot_general | solution.py:260
  94.5 1.7 %fusion.33 = (bf16[1,8,640,128]{3,2,1,0:T(8,128)(2,1)}, bf16[1,8,640,128]{3,2,1,0:T(8,128)(2,1)}, bf16[1,8,640,128]{3,2,1,0:T(8,128)(2,1)S(1)}) fusion(bf16[3,8,640,128]{3,2,1,0:T(8,128)(2,1)S(1)} %convert_bitcast_fusion), kind=kLoop, calls=%fused_computation.64 | loop fusion | bytes 7864320 | tf_op jit(solution)/shard_map/slice | solution.py:264
  96.2 5.4 %fusion.34 = (f32[8,8,128]{2,1,0:T(8,128)S(1)}, f32[8,8,128,128]{2,3,1,0:T(8,128)}) fusion(bf16[8,8,80,128]{3,2,1,0:T(8,128)(2,1)} %bitcast.65, bf16[8,8,80,128]{3,2,1,0:T(8,128)(2,1)} %bitcast.64), kind=kOutput, calls=%fused_computation.65 | convolution fusion | flops 170918016 | bytes 6848512 | tf_op jit(solution)/shard_map/sub | solution.py:266
  101.6 3.0 %fusion.18 = bf16[8,8,80,128]{3,2,1,0:T(8,128)(2,1)S(1)} fusion(bf16[8,8,80,128]{3,2,1,0:T(8,128)(2,1)S(1)} %bitcast.63, f32[8,8,128,128]{2,3,1,0:T(8,128)} %get-tuple-element.19, f32[8,8,128]{2,1,0:T(8,128)S(1)} %get-tuple-element.18), kind=kOutput, calls=%fused_computation.21 | convolution fusion | flops 170524672 | bytes 6848512 | tf_op jit(solution)/shard_map/rhts,rhes->rhet/dot_general | solution.py:267
  104.6 3.7 %fusion.6 = bf16[8,1280,128]{2,1,0:T(8,128)(2,1)} fusion(bf16[1280,640,1]{1,0,2:T(8,128)(2,1)S(1)} %bitcast.59, bf16[8,640,128]{2,1,0:T(8,128)(2,1)S(1)} %bitcast.68), kind=kOutput, calls=%fused_computation.13 | convolution fusion | flops 1679032320 | bytes 5570560 | tf_op jit(solution)/shard_map/cep,fe->cfp/dot_general | solution.py:269
  108.4 0.0 copy-start.3
  108.4 0.0 reduce-scatter.2.cloned.1.call-update
  108.4 36.2 %reduce-scatter.2.cloned.1.call-done = bf16[8,640,128]{2,1,0:T(8,128)(2,1)} async-done(((bf16[8,1280,128]{2,1,0:T(8,128)(2,1)}), bf16[8,640,128]{2,1,0:T(8,128)(2,1)}) %reduce-scatter.2.cloned.1.call-update) | async-done | bytes 1310736 | tf_op jit(solution)/shard_map/reduce_scatter | solution.py:270
  144.6 0.0 copy-done.3
  144.6 2.7 %fusion.19 = bf16[1,8,640,128]{3,2,1,0:T(8,128)(2,1)} fusion(bf16[8,640,128]{2,1,0:T(8,128)(2,1)} %reduce-scatter.2.cloned.1.call-done, bf16[8,1280,128]{2,1,0:T(8,128)(2,1)S(1)} %copy-done.3, s32[]{:T(128)S(6)} %select_n.99), kind=kLoop, calls=%fused_computation.22 | loop fusion | flops 2621440 | bytes 3932164 | tf_op jit(solution)/shard_map/broadcast_in_dim | solution.py:273
  (4 shorter events, 0.0 us)
Async XLA Ops:
  6.5 138.0 %reduce-scatter.2.cloned.1.call-start = ((), (), s32[]{:S(2)}) async-start(), calls=%async_computation.1 | async-start | bytes 3932160 | tf_op jit(solution)/shard_map/reduce_scatter | solution.py:270
  10.2 1.3 copy-start
  11.5 1.0 copy-start.1
  84.6 3.2 %copy-start.2 = (bf16[8,1280,128]{2,1,0:T(8,128)(2,1)S(1)}, bf16[8,1280,128]{2,1,0:T(8,128)(2,1)}, u32[]{:S(2)}) copy-start(bf16[8,1280,128]{2,1,0:T(8,128)(2,1)} %get-tuple-element.8) | copy-start | bytes 7864324
  108.4 36.2 %copy-start.3 = (bf16[8,1280,128]{2,1,0:T(8,128)(2,1)S(1)}, bf16[8,1280,128]{2,1,0:T(8,128)(2,1)}, u32[]{:S(2)}) copy-start(bf16[8,1280,128]{2,1,0:T(8,128)(2,1)} %get-tuple-element.8) | copy-start | bytes 7864324
Sparse Core Ops, SparseCore 0:
  108.5 36.0 reduce-scatter.1

commit v2 on v1

--- a/solution.py
+++ b/solution.py
@@ -31,15 +31,20 @@
     )
 
 
-def gather_kernel(sizes, *refs):
+def encode_kernel(sizes, *refs):
     nd, nb, nt = sizes
     bits = bits_of(nb)
     ns = len(bits)
-    tab, tiles, wq_in, wo_in, gath, wq, wo = refs[:7]
-    sends, recvs = refs[7 : 7 + ns], refs[7 + ns : 7 + 2 * ns]
-    t_send, t_recv, y_send, y_recv, w_send, w_recv, d_send, d_recv = refs[7 + 2 * ns :]
+    tab, tiles, wq_in, wo_in, out = refs[:5]
+    sends, recvs = refs[5 : 5 + ns], refs[5 + ns : 5 + 2 * ns]
+    gath, wq, wo, wide_q, wide_o, normed, qkv, context, own, p_out, p_in = refs[
+        5 + 2 * ns : 16 + 2 * ns
+    ]
+    t_send, t_recv, y_send, y_recv, w_send, w_recv, d_send, d_recv, p_send, p_recv = refs[
+        16 + 2 * ns :
+    ]
     z, b, t = lax.axis_index("dp"), lax.axis_index("bal"), lax.axis_index("tensor")
-    slices = tiles.shape[1]
+    _, slices, patches = tiles.shape
     chunks = CAP // CHUNK
 
     barrier = pltpu.get_barrier_semaphore()
@@ -151,10 +156,10 @@
             return carry
 
         lax.fori_loop(1, nd, first, 0)
-    for s in range(1, ns + 1):
-        for a in range(2):
-
-            def further(j, carry, a=a, s=s):
+    def finish(a):
+        for s in range(1, ns + 1):
+
+            def further(j, carry, s=s):
                 for e in range(1 << (s - 1)):
                     doubled(j, a, s - 1, e).wait_recv()
                 if s < ns:
@@ -167,7 +172,96 @@
     for c in range(chunks):
         for j in range(1, nt):
             y_copy(c, j).wait_recv()
+    for i in range(CAP):
+        values = gath[i].astype(jnp.float32)
+        center = values - jnp.mean(values, axis=0, keepdims=True)
+        spread_of = jnp.mean(center * center, axis=0, keepdims=True)
+        normed[:, i * patches : (i + 1) * patches] = (
+            center * lax.rsqrt(spread_of + EPSILON)
+        ).astype(normed.dtype)
+
+    finish(0)
+    rows = wide_q.shape[1] // nd
+    part_rows = wq.shape[2]
+    for y in range(nd):
+        for e in range(nb):
+            at = 0
+            while at < part_rows:
+                k, row = divmod(e * part_rows + at, rows)
+                size = min(rows - row, part_rows - at)
+                wide_q[k, y * rows + row : y * rows + row + size] = wq[y, e, at : at + size]
+                at += size
+
+    def project(k, carry):
+        qkv[k] = lax.dot_general(
+            wide_q[k], normed[...], (((0,), (0,)), ((), ())), preferred_element_type=jnp.float32
+        ).astype(qkv.dtype)
+        return carry
+
+    lax.fori_loop(0, 3, project, 0)
+    finish(1)
+    part_rows = wo.shape[2]
+    for y in range(nd):
+        for e in range(nb):
+            start = (y * nb + e) * part_rows
+            wide_o[start : start + part_rows] = wo[y, e]
+
+    def p_copy(c, j):
+        part = pl.ds(c * CHUNK, CHUNK)
+        return remote(
+            p_out.at[j - 1, part], p_in.at[j - 1, part], p_send.at[c, j], p_recv.at[c, j],
+            tensor=(t + j) % nt,
+        )
+
+    heads = slices // HDIM
+
+    def partial(target):
+        block = wide_o[pl.ds(pl.multiple_of(target * slices, 16), slices), :]
+        return jnp.dot(block, context[...], preferred_element_type=jnp.float32).astype(own.dtype)
+
+    def encode(c, carry):
+        for i in range(CHUNK):
+            here = pl.ds(pl.multiple_of((c * CHUNK + i) * patches, patches), patches)
+            for h in range(heads):
+                span = slice(h * HDIM, (h + 1) * HDIM)
+                scores = lax.dot_general(
+                    qkv[1, span, here], qkv[0, span, here], (((0,), (0,)), ((), ())),
+                    preferred_element_type=jnp.float32,
+                ) * HDIM ** (-0.5)
+                powers = jnp.exp(scores - jnp.max(scores, axis=0, keepdims=True))
+                probs = powers * (1.0 / jnp.sum(powers, axis=0, keepdims=True))
+                context[span, i * patches : (i + 1) * patches] = jnp.dot(
+                    qkv[2, span, here], probs.astype(qkv.dtype), preferred_element_type=jnp.float32
+                ).astype(context.dtype)
+        for j in range(1, nt):
+            block = partial((t + j) % nt)
+            for i in range(CHUNK):
+                p_out[j - 1, c * CHUNK + i] = block[:, i * patches : (i + 1) * patches]
+            p_copy(c, j).start()
+        block = partial(t)
+        for i in range(CHUNK):
+            own[c * CHUNK + i] = block[:, i * patches : (i + 1) * patches]
+        return carry
+
+    lax.fori_loop(0, chunks, encode, 0)
+
+    def close(c, carry):
+        for j in range(1, nt):
+            p_copy(c, j).wait_recv()
+        for i in range(CHUNK):
+            at = c * CHUNK + i
+            total = gath[at, mine, :].astype(jnp.float32) + own[at].astype(jnp.float32)
+            for j in range(1, nt):
+                total = total + p_in[j - 1, at].astype(jnp.float32)
+            out[at] = total.astype(out.dtype)
+        return carry
+
+    lax.fori_loop(0, chunks, close, 0)
+
+    for c in range(chunks):
+        for j in range(1, nt):
             y_copy(c, j).wait_send()
+            p_copy(c, j).wait_send()
     for s, m in enumerate(bits):
         for slot in range(nb >> (s + 1)):
             for c in range(chunks):
@@ -184,43 +278,52 @@
         lax.fori_loop(1, nd, drain, 0)
 
 
-def gather_all(table, tiles, qkv_weight, out_weight):
+def encode_all(table, tiles, qkv_weight, out_weight):
     nd, nb, nt = (lax.axis_size(name) for name in ("dp", "bal", "tensor"))
     ns = len(bits_of(nb))
     slots, slices, patches = tiles.shape
-    columns = qkv_weight.shape[-1]
+    kinds, rows, columns = qkv_weight.shape
     wq = qkv_weight.reshape(nb, -1, columns)
     wo = out_weight.reshape(nb, -1, columns)
     chunks = CAP // CHUNK
     dtype = tiles.dtype
     vmem = pl.BlockSpec(memory_space=pltpu.VMEM)
     dma = pltpu.SemaphoreType.DMA
-    buffers = [pltpu.VMEM((nb >> (s + 1), CAP, slices, patches), dtype) for s in range(ns)]
-    gathered, full_qkv, full_out = pl.pallas_call(
-        functools.partial(gather_kernel, (nd, nb, nt)),
-        out_shape=(
-            jax.ShapeDtypeStruct((CAP, nt * slices, patches), dtype),
-            jax.ShapeDtypeStruct((nd,) + wq.shape, dtype),
-            jax.ShapeDtypeStruct((nd,) + wo.shape, dtype),
-        ),
+
+    def space(*shape):
+        return pltpu.VMEM(shape, dtype)
+
+    buffers = [space(nb >> (s + 1), CAP, slices, patches) for s in range(ns)]
+    return pl.pallas_call(
+        functools.partial(encode_kernel, (nd, nb, nt)),
+        out_shape=jax.ShapeDtypeStruct((CAP, slices, patches), dtype),
         in_specs=[pl.BlockSpec(memory_space=pltpu.SMEM), vmem, vmem, vmem],
-        out_specs=(vmem, vmem, vmem),
+        out_specs=vmem,
         scratch_shapes=buffers
         + buffers
+        + [
+            space(CAP, nt * slices, patches),
+            space(nd, *wq.shape),
+            space(nd, *wo.shape),
+            space(kinds, nd * rows, columns),
+            space(nt * slices, columns),
+            space(nt * slices, CAP * patches),
+            space(kinds, columns, CAP * patches),
+            space(columns, CHUNK * patches),
+            space(CAP, slices, patches),
+            space(max(nt - 1, 1), CAP, slices, patches),
+            space(max(nt - 1, 1), CAP, slices, patches),
+        ]
         + [dma((ns, max(nb // 2, 1), chunks))] * 2
         + [dma((chunks, nt))] * 2
         + [dma((2, nd))] * 2
-        + [dma((2, nd, nb))] * 2,
+        + [dma((2, nd, nb))] * 2
+        + [dma((chunks, nt))] * 2,
         compiler_params=pltpu.CompilerParams(
-            collective_id=0, has_side_effects=True, vmem_limit_bytes=50 * 1024 * 1024
+            collective_id=0, has_side_effects=True, vmem_limit_bytes=60 * 1024 * 1024
         ),
-        name="gather_all",
+        name="encode_all",
     )(table, tiles, wq, wo)
-    return (
-        gathered,
-        full_qkv.reshape((nd,) + qkv_weight.shape),
-        full_out.reshape((-1, columns)),
-    )
 
 
 def route(counts, ordering, slot_count):
@@ -241,36 +344,10 @@
     return jnp.stack(rows)
 
 
-def normalize(tile_rows):
-    values = tile_rows.astype(jnp.float32)
-    center = values - jnp.mean(values, axis=1, keepdims=True)
-    spread = jnp.mean(center * center, axis=1, keepdims=True)
-    return (center * lax.rsqrt(spread + EPSILON)).astype(jnp.bfloat16)
-
-
 def local(tiles, tile_counts, doc_order, qkv_weight, out_weight):
     own_tiles = tiles[0, 0]
-    slot_count, slices, patches = own_tiles.shape
-    table = route(tile_counts[0], doc_order[0], slot_count)
-    gathered, full_qkv, full_out = gather_all(table, own_tiles, qkv_weight, out_weight)
-    t = lax.axis_index("tensor")
-    chosen = lax.dynamic_slice_in_dim(gathered, t * slices, slices, axis=1)
-    normed = normalize(gathered)
-    full_qkv = full_qkv.transpose(1, 0, 2, 3).reshape(3, -1, slices)
-    projected = jnp.einsum("cdp,kdf->kcfp", normed, full_qkv, preferred_element_type=jnp.float32)
-    head_count = slices // HDIM
-    projected = projected.astype(jnp.bfloat16).reshape(3, CAP, head_count, HDIM, patches)
-    scores = jnp.einsum(
-        "rhet,rhes->rhts", projected[0], projected[1], preferred_element_type=jnp.float32
-    ) * HDIM ** (-0.5)
-    probs = jax.nn.softmax(scores, axis=-1).astype(jnp.bfloat16)
-    context = jnp.einsum("rhts,rhes->rhet", probs, projected[2], preferred_element_type=jnp.float32)
-    context = context.astype(jnp.bfloat16).reshape(CAP, slices, patches)
-    partial_value = jnp.einsum("cep,fe->cfp", context, full_out, preferred_element_type=jnp.float32)
-    summed = lax.psum_scatter(
-        partial_value.astype(jnp.bfloat16), "tensor", scatter_dimension=1, tiled=True
-    ).astype(jnp.float32)
-    return (chosen.astype(jnp.float32) + summed).astype(jnp.bfloat16)[None]
+    table = route(tile_counts[0], doc_order[0], own_tiles.shape[0])
+    return encode_all(table, own_tiles, qkv_weight, out_weight)[None]
 
 
 def solution(mesh):

time: 155 us -> 113 us (0.73)
  waiting for transfers between devices: 36.2 us -> 0 us
  Pallas kernels: 72.1 us -> 106 us
  matrix products: 17.7 us -> 0 us
  between operations: 13.5 us -> 0.02 us
  local copies, waits for them, and re-layouts: 7.23 us -> 2.47 us
  other arithmetic: 7.42 us -> 4.24 us
    reduce_scatter x1 -> x0, waiting for transfers between devices: 36.2 us -> none  [local(): lax.psum_scatter(partial_value.astype(jnp.bfloat16), 'tensor', scatter_di...]
    pallas_call x1, Pallas kernels: 72.1 us -> 106 us  [encode_all(): pl.pallas_call(functools.partial(encode_kernel, (nd, nb, nt)), out_shape=...]
    dot_general x3 -> x0, matrix products: 12.3 us -> none  [the longest x1 5.57 us: local(): jnp.einsum('cdp,kdf->kcfp', normed, full_qkv, preferred_element_type=jnp....]
    sub x1 -> x0, matrix products: 5.35 us -> none  [local(): probs = jax.nn.softmax(scores, axis=-1).astype(jnp.bfloat16)]
    reshape x1 -> x0, local copies, waits for them, and re-layouts: 2.99 us -> none  [gather_all(): full_qkv.reshape((nd,) + qkv_weight.shape)]
    broadcast_in_dim x1 -> x0, other arithmetic: 2.71 us -> none  [local(): return (chosen.astype(jnp.float32) + summed).astype(jnp.bfloat16)[None]]
    slice x1 -> x0, local copies, waits for them, and re-layouts: 1.74 us -> none  [local(): projected[1]]
  transfers between devices with their start and end apart: 1 -> 0, of which waited for: 1 -> 0; matrix products, arithmetic and copies ran while one was open for 0% -> 0% of each run, Pallas kernels for 0% -> 0%
where the time goes in v2:
time: 113 us; the launch traced here: 112 us
  Pallas kernels  106 us (94%)
  other arithmetic  4.24 us (4%)
  local copies, waits for them, and re-layouts  2.47 us (2%)
    pallas_call x1, Pallas kernels, encode_all(): pl.pallas_call(functools.partial(encode_kernel, (nd, nb, nt)), out_shape=...  106 us
    unnamed x1, local copies, waits for them, and re-layouts  2.47 us

profile of v2, /device:TPU:0, one launch (start us, length us, event | category | flops | bytes accessed | tf_op | source)
XLA Modules:
  0.0 112.4 jit_solution(17727077189285308995)
XLA Ops:
  0.0 0.8 select_reduce_fusion.2
  0.8 0.8 select_reduce_fusion.1
  1.6 1.3 %fusion.8 = (s32[]{:T(128)}, s32[4]{0:T(128)S(1)}) fusion(s32[4]{0:T(128)S(1)} %select_reduce_fusion.1, s32[]{:T(128)S(6)} %axis_index.15, s32[1,4]{1,0:T(1,128)} %param.6), kind=kLoop, calls=%fused_computation.32 | loop fusion | flops 15 | bytes 56 | tf_op jit(solution)/shard_map/reduce_sum | solution.py:336
  2.9 0.1 select_reduce_fusion
  3.0 0.7 and_select_fusion.2
  3.7 0.6 pad_add_fusion.refs_0_
  4.3 105.6 %encode_all.1 = bf16[8,640,128]{2,1,0:T(8,128)(2,1)} custom-call(s32[3,32]{1,0:T(4,128)} %pad_add_fusion.refs_0_, bf16[16,640,128]{2,1,0:T(8,128)(2,1)} %bitcast.25, bf16[4,240,640]{2,1,0:T(8,128)(2,1)} %bitcast.26, bf16[4,80,640]{2,1,0:T(8,128)(2,1)} %bitcast.27), custom_call_target="tpu_custom_call" | custom-call | tf_op jit(solution)/shard_map/encode_all/pallas_call | solution.py:297
  109.9 2.5 %copy.7 = bf16[1,8,640,128]{3,2,1,0:T(8,128)(2,1)} copy(bf16[1,8,640,128]{3,2,1,0:T(8,128)(2,1)} %bitcast.24) | data formatting | bytes 2621440
  (1 shorter events, 0.0 us)

commit v3 on v2

--- a/solution.py
+++ b/solution.py
@@ -35,14 +35,12 @@
     nd, nb, nt = sizes
     bits = bits_of(nb)
     ns = len(bits)
-    tab, tiles, wq_in, wo_in, out = refs[:5]
-    sends, recvs = refs[5 : 5 + ns], refs[5 + ns : 5 + 2 * ns]
-    gath, wq, wo, wide_q, wide_o, normed, qkv, context, own, p_out, p_in = refs[
-        5 + 2 * ns : 16 + 2 * ns
-    ]
-    t_send, t_recv, y_send, y_recv, w_send, w_recv, d_send, d_recv, p_send, p_recv = refs[
-        16 + 2 * ns :
-    ]
+    counts, order, tiles, wq_in, wo_in, out = refs[:6]
+    sends, recvs = refs[6 : 6 + ns], refs[6 + ns : 6 + 2 * ns]
+    gath, wq, wo, wide_o, normed, qkv, context, own, p_out, p_in = refs[6 + 2 * ns : 16 + 2 * ns]
+    sems = refs[16 + 2 * ns :]
+    t_send, t_recv, y_send, y_recv, w_send, w_recv, d_send, d_recv, p_send, p_recv = sems[:10]
+    l_send, l_recv, h_send, h_recv = sems[10:]
     z, b, t = lax.axis_index("dp"), lax.axis_index("bal"), lax.axis_index("tensor")
     _, slices, patches = tiles.shape
     chunks = CAP // CHUNK
@@ -60,21 +58,50 @@
     lax.fori_loop(1, nd, greet, 0)
     pl.semaphore_wait(barrier, ns + nt - 1 + nd - 1)
 
-    pairs = ((wq_in, wq), (wo_in, wo))
-
-    def spread(j, a):
-        src, dst = pairs[a]
-        return remote(
-            src.at[b], dst.at[z, b], w_send.at[a, j], w_recv.at[a, j], dp=(z + j) % nd
+    def spread(j):
+        return remote(wo_in.at[b], wo.at[z, b], w_send.at[j], w_recv.at[j], dp=(z + j) % nd)
+
+    part_count = wq.shape[2]
+    part = b % part_count
+
+    def line(way, s):
+        step = 1 - 2 * way
+        src = z - step * s
+        there = z + step
+        valid = (src >= 0) & (src < nd) & (there >= 0) & (there < nd)
+        dst = wq.at[:, jnp.clip(src, 0, nd - 1), part]
+        origin = wq_in.at[:, part] if isinstance(s, int) and s == 0 else dst
+        copy = remote(
+            origin, dst, l_send.at[way, s], l_recv.at[way, s], dp=jnp.clip(there, 0, nd - 1)
         )
-
-    for a in range(2):
-
-        def start_spread(j, carry, a=a):
-            spread(j, a).start()
-            return carry
-
-        lax.fori_loop(1, nd, start_spread, 0)
+        return valid, copy
+
+    def arrival(way, s):
+        step = 1 - 2 * way
+        src = z - step * (s + 1)
+        valid = (src >= 0) & (src < nd)
+        at = wq.at[:, jnp.clip(src, 0, nd - 1), part]
+        here = remote(
+            at, at, l_send.at[way, s], l_recv.at[way, s], dp=jnp.clip(z + step, 0, nd - 1)
+        )
+        half = remote(at, at, h_send.at[way, s], h_recv.at[way, s], bal=flip(b, 1))
+        return valid, here, half
+
+    for way in range(2):
+        valid, copy = line(way, 0)
+        pl.when(valid)(copy.start)
+
+    def hop(s):
+        for way in range(2):
+            valid, here, half = arrival(way, s)
+            further, copy = line(way, s + 1)
+
+            @pl.when(valid)
+            def _(here=here, half=half, further=further, copy=copy):
+                here.wait_recv()
+                pl.when(further)(copy.start)
+                if part_count > 1:
+                    half.start()
 
     def tile_copy(s, slot, c):
         part = pl.ds(c * CHUNK, CHUNK)
@@ -93,12 +120,29 @@
         for q in range(s):
             tile_copy(q, slot_of(q, r), c).wait_recv()
 
+    docs = order.shape[1]
+    placed = [order[0, p] for p in range(docs)]
+    edges = [jnp.int32(0)]
+    for doc in placed:
+        edges.append(edges[-1] + counts[0, doc])
+    own_start = jnp.int32(0)
+    for p in range(docs):
+        own_start = own_start + jnp.where(placed[p] == b, edges[p], 0)
+
     def current(s, r, i):
-        value = tiles[tab[0, r * CAP + i]]
+        block = b
+        for m in bits:
+            if r & m:
+                block = flip(block, m)
+        packed = block * CAP + i
+        owner = jnp.int32(0)
+        for p in range(docs):
+            inside = (edges[p] <= packed) & (packed < edges[p + 1])
+            owner = owner + jnp.where(inside, placed[p], 0)
+        value = tiles[jnp.clip(packed - own_start, 0, tiles.shape[0] - 1)]
         for q in range(s):
-            value = lax.select(
-                tab[1 + q, r * CAP + i] != 0, recvs[q][slot_of(q, r), i], value
-            )
+            apart = (owner // bits[q]) % 2 != (b // bits[q]) % 2
+            value = lax.select(apart, recvs[q][slot_of(q, r), i], value)
         return value
 
     for s, m in enumerate(bits):
@@ -121,6 +165,7 @@
         part = gath.at[pl.ds(c * CHUNK, CHUNK), mine, :]
         return remote(part, part, y_send.at[c, j], y_recv.at[c, j], tensor=(t + j) % nt)
 
+    early = min((chunks + 1) // 2, nd - 2)
     for c in range(chunks):
         wait_for(ns, 0, c)
 
@@ -131,48 +176,44 @@
         lax.fori_loop(c * CHUNK, (c + 1) * CHUNK, settle, 0)
         for j in range(1, nt):
             y_copy(c, j).start()
-
-    for a in range(2):
-        src, dst = pairs[a]
-        dst[z] = src[...]
-
-    def doubled(j, a, s, e):
+        if c % 2 == 0 and c // 2 < early:
+            hop(c // 2)
+
+    def start_spread(j, carry):
+        spread(j).start()
+        return carry
+
+    lax.fori_loop(1, nd, start_spread, 0)
+    wq[:, z] = wq_in[...]
+    wo[z] = wo_in[...]
+
+    def doubled(j, s, e):
         src = (z + nd - j) % nd
         held = b
         for q in range(s):
             if (e >> q) & 1:
                 held = flip(held, bits[ns - 1 - q])
-        dst = pairs[a][1].at[src, held]
+        dst = wo.at[src, held]
         at = (1 << s) - 1 + e
         return remote(
-            dst, dst, d_send.at[a, j, at], d_recv.at[a, j, at], bal=flip(b, bits[ns - 1 - s])
+            dst, dst, d_send.at[j, at], d_recv.at[j, at], bal=flip(b, bits[ns - 1 - s])
         )
 
-    for a in range(2):
-
-        def first(j, carry, a=a):
-            spread(j, a).wait_recv()
-            doubled(j, a, 0, 0).start()
+    def finish(s):
+        def further(j, carry):
+            if s == 0:
+                spread(j).wait_recv()
+            else:
+                for e in range(1 << (s - 1)):
+                    doubled(j, s - 1, e).wait_recv()
+            if s < ns:
+                for e in range(1 << s):
+                    doubled(j, s, e).start()
             return carry
 
-        lax.fori_loop(1, nd, first, 0)
-    def finish(a):
-        for s in range(1, ns + 1):
-
-            def further(j, carry, s=s):
-                for e in range(1 << (s - 1)):
-                    doubled(j, a, s - 1, e).wait_recv()
-                if s < ns:
-                    for e in range(1 << s):
-                        doubled(j, a, s, e).start()
-                return carry
-
-            lax.fori_loop(1, nd, further, 0)
-
-    for c in range(chunks):
-        for j in range(1, nt):
-            y_copy(c, j).wait_recv()
-    for i in range(CAP):
+        lax.fori_loop(1, nd, further, 0)
+
+    def normalize(i):
         values = gath[i].astype(jnp.float32)
         center = values - jnp.mean(values, axis=0, keepdims=True)
         spread_of = jnp.mean(center * center, axis=0, keepdims=True)
@@ -180,26 +221,40 @@
             center * lax.rsqrt(spread_of + EPSILON)
         ).astype(normed.dtype)
 
+    for c in range(chunks):
+        for j in range(1, nt):
+            y_copy(c, j).wait_recv()
+        for i in range(c * CHUNK, (c + 1) * CHUNK):
+            normalize(i)
+
+    def rest(s, carry):
+        hop(s)
+        return carry
+
+    lax.fori_loop(early, nd - 1, rest, 0)
     finish(0)
-    rows = wide_q.shape[1] // nd
-    part_rows = wq.shape[2]
-    for y in range(nd):
-        for e in range(nb):
-            at = 0
-            while at < part_rows:
-                k, row = divmod(e * part_rows + at, rows)
-                size = min(rows - row, part_rows - at)
-                wide_q[k, y * rows + row : y * rows + row + size] = wq[y, e, at : at + size]
-                at += size
+
+    def halves(s, carry):
+        for way in range(2):
+            valid, _, half = arrival(way, s)
+            pl.when(valid)(half.wait_recv)
+        return carry
+
+    if part_count > 1:
+        lax.fori_loop(0, nd - 1, halves, 0)
 
     def project(k, carry):
         qkv[k] = lax.dot_general(
-            wide_q[k], normed[...], (((0,), (0,)), ((), ())), preferred_element_type=jnp.float32
+            wq[k].reshape(normed.shape[0], slices),
+            normed[...],
+            (((0,), (0,)), ((), ())),
+            preferred_element_type=jnp.float32,
         ).astype(qkv.dtype)
         return carry
 
     lax.fori_loop(0, 3, project, 0)
-    finish(1)
+    for s in range(1, ns + 1):
+        finish(s)
     part_rows = wo.shape[2]
     for y in range(nd):
         for e in range(nb):
@@ -266,24 +321,33 @@
         for slot in range(nb >> (s + 1)):
             for c in range(chunks):
                 tile_copy(s, slot, c).wait_send()
-    for a in range(2):
-
-        def drain(j, carry, a=a):
-            spread(j, a).wait_send()
-            for s in range(ns):
-                for e in range(1 << s):
-                    doubled(j, a, s, e).wait_send()
-            return carry
-
-        lax.fori_loop(1, nd, drain, 0)
-
-
-def encode_all(table, tiles, qkv_weight, out_weight):
+    def drain(j, carry):
+        spread(j).wait_send()
+        for s in range(ns):
+            for e in range(1 << s):
+                doubled(j, s, e).wait_send()
+        return carry
+
+    lax.fori_loop(1, nd, drain, 0)
+
+    def drain_line(s, carry):
+        for way in range(2):
+            valid, copy = line(way, s)
+            pl.when(valid)(copy.wait_send)
+            valid, _, half = arrival(way, s)
+            if part_count > 1:
+                pl.when(valid)(half.wait_send)
+        return carry
+
+    lax.fori_loop(0, nd - 1, drain_line, 0)
+
+
+def encode_all(counts, ordering, tiles, qkv_weight, out_weight):
     nd, nb, nt = (lax.axis_size(name) for name in ("dp", "bal", "tensor"))
     ns = len(bits_of(nb))
     slots, slices, patches = tiles.shape
     kinds, rows, columns = qkv_weight.shape
-    wq = qkv_weight.reshape(nb, -1, columns)
+    wq = qkv_weight.reshape(kinds, min(nb, 2), -1, columns)
     wo = out_weight.reshape(nb, -1, columns)
     chunks = CAP // CHUNK
     dtype = tiles.dtype
@@ -297,15 +361,14 @@
     return pl.pallas_call(
         functools.partial(encode_kernel, (nd, nb, nt)),
         out_shape=jax.ShapeDtypeStruct((CAP, slices, patches), dtype),
-        in_specs=[pl.BlockSpec(memory_space=pltpu.SMEM), vmem, vmem, vmem],
+        in_specs=[pl.BlockSpec(memory_space=pltpu.SMEM)] * 2 + [vmem] * 3,
         out_specs=vmem,
         scratch_shapes=buffers
         + buffers
         + [
             space(CAP, nt * slices, patches),
-            space(nd, *wq.shape),
+            space(kinds, nd, *wq.shape[1:]),
             space(nd, *wo.shape),
-            space(kinds, nd * rows, columns),
             space(nt * slices, columns),
             space(nt * slices, CAP * patches),
             space(kinds, columns, CAP * patches),
@@ -316,38 +379,20 @@
         ]
         + [dma((ns, max(nb // 2, 1), chunks))] * 2
         + [dma((chunks, nt))] * 2
-        + [dma((2, nd))] * 2
-        + [dma((2, nd, nb))] * 2
-        + [dma((chunks, nt))] * 2,
+        + [dma((nd,))] * 2
+        + [dma((nd, nb))] * 2
+        + [dma((chunks, nt))] * 2
+        + [dma((2, nd))] * 4,
         compiler_params=pltpu.CompilerParams(
             collective_id=0, has_side_effects=True, vmem_limit_bytes=60 * 1024 * 1024
         ),
         name="encode_all",
-    )(table, tiles, wq, wo)
-
-
-def route(counts, ordering, slot_count):
-    nb, b = lax.axis_size("bal"), lax.axis_index("bal")
-    doc_ids = jnp.arange(counts.shape[0], dtype=jnp.int32)
-    position = jnp.sum(
-        jnp.where(ordering[None, :] == doc_ids[:, None], doc_ids[None, :], 0), axis=1
-    )
-    starts = jnp.sum(jnp.where(position[None, :] < position[:, None], counts[None, :], 0), axis=1)
-    own_start = jnp.sum(jnp.where(doc_ids == b, starts, 0))
-    relative = jnp.arange(nb * CAP, dtype=jnp.int32)
-    packed = ((relative // CAP) ^ b) * CAP + relative % CAP
-    inside = (starts[:, None] <= packed[None, :]) & (packed[None, :] < (starts + counts)[:, None])
-    owner = jnp.sum(jnp.where(inside, doc_ids[:, None], 0), axis=0)
-    rows = [jnp.clip(packed - own_start, 0, slot_count - 1)]
-    for m in bits_of(nb):
-        rows.append(((owner ^ b) // m) % 2)
-    return jnp.stack(rows)
+    )(counts, ordering, tiles, wq, wo)
 
 
 def local(tiles, tile_counts, doc_order, qkv_weight, out_weight):
     own_tiles = tiles[0, 0]
-    table = route(tile_counts[0], doc_order[0], own_tiles.shape[0])
-    return encode_all(table, own_tiles, qkv_weight, out_weight)[None]
+    return encode_all(tile_counts, doc_order, own_tiles, qkv_weight, out_weight)[None]
 
 
 def solution(mesh):

time: 113 us -> 101 us (0.89)
  Pallas kernels: 106 us -> 98.8 us
  other arithmetic: 4.24 us -> 0 us
    pallas_call x1, Pallas kernels: 106 us -> 98.8 us  [encode_all(): pl.pallas_call(functools.partial(encode_kernel, (nd, nb, nt)), out_shape=...]
    reduce_sum x4 -> x0, other arithmetic: 2.99 us -> none  [the longest x1 1.29 us: route(): own_start = jnp.sum(jnp.where(doc_ids == b, starts, 0))]
where the time goes in v3:
time: 101 us
  Pallas kernels  98.8 us (98%)
  local copies, waits for them, and re-layouts  2.47 us (2%)
    pallas_call x1, Pallas kernels, encode_all(): pl.pallas_call(functools.partial(encode_kernel, (nd, nb, nt)), out_shape=...  98.8 us
    unnamed x1, local copies, waits for them, and re-layouts  2.47 us

profile of v3, /device:TPU:0, one launch (start us, length us, event | category | flops | bytes accessed | tf_op | source)
XLA Modules:
  0.0 101.3 jit_solution(3337912520541579795)
XLA Ops:
  0.0 98.8 %encode_all.1 = bf16[8,640,128]{2,1,0:T(8,128)(2,1)} custom-call(s32[1,4]{1,0:T(1,128)} %refs_0_.1, s32[1,4]{1,0:T(1,128)} %refs_1_.1, bf16[16,640,128]{2,1,0:T(8,128)(2,1)} %bitcast.5, bf16[3,2,160,640]{3,2,1,0:T(8,128)(2,1)} %bitcast.6, bf16[4,80,640]{2,1,0:T(8,128)(2,1)} %bitcast.7), custom_call_target="tpu_custom_call" | custom-call | tf_op jit(solution)/shard_map/encode_all/pallas_call | solution.py:361
  98.8 2.5 %copy.7 = bf16[1,8,640,128]{3,2,1,0:T(8,128)(2,1)} copy(bf16[1,8,640,128]{3,2,1,0:T(8,128)(2,1)} %bitcast.4) | data formatting | bytes 2621440
